TPU v7x, 32 devices: a whole 2x2x4 slice. The times are simulated.
32 devices in a mesh: sky: 4 (over x, core), tm: 8 (over z, y).
Axes of the slice: x: 2, y: 2, z: 4, core: 2. Of those that a mesh axis runs over, the one named last changes fastest.
Arguments:
- attitude: float32 [4, 8, 512], P(None, 'tm', 'sky'), may hold values from -6 to 6
- slot_time: float32 [262144], P(('sky', 'tm')), may hold values from -1 to 1
- slot_parallax: float32 [262144], P(('sky', 'tm')), may hold values from -1 to 1
- slot_observed: float32 [262144], P(('sky', 'tm')), may hold values from -6 to 6
- slot_phase: float32 [262144], P(('sky', 'tm')), may hold values from 0 to 1
- slot_knot: int32 [262144], P(('sky', 'tm')), may hold values from 0 to 508
- block_source: int32 [8192], P(('sky', 'tm')), may hold values from 0 to 63
- block_count: int32 [8192], P(('sky', 'tm')), may hold values from 1 to 32
- prior: float32 [5, 256], P(None, ('sky', 'tm')), may hold values from 0.5 to 4
Outputs:
- update: float32 [5, 256], P(None, ('sky', 'tm'))
Inputs may be any that keep to these rules, and one draw needn't show every extreme that they name: The four knots from slot_knot on lie in the transit's time group of 512 knots. `block_source`: an index into the 64 sources of the block's own sky sector.
All inputs are finite; a program needn't handle non-finite values.
Results may differ from a plain program's by a relative error of at most 0.0003.
Values sent between devices are 32-bit elements; how exact they have to be, the bound alone decides.
A program may use at most 64 MiB of HBM per device.

v0:
```python
import functools

import jax
import jax.numpy as jnp
from jax import lax
from jax.experimental import pallas as pl
from jax.experimental.pallas import tpu as pltpu
from jax.sharding import PartitionSpec as P

PAIR_LIST = [(i, j) for i in range(5) for j in range(i, 5)]
MESH = pl.DeviceIdType.MESH
LANES = 128
ROWS = 32


def lane_gather(row, index):
    wide = jnp.broadcast_to(row, index.shape)
    return jnp.take_along_axis(wide, index, axis=1, mode="promise_in_bounds")


def split3(value):
    high = value.astype(jnp.bfloat16)
    rest = value - high.astype(jnp.float32)
    mid = rest.astype(jnp.bfloat16)
    low = (rest - mid.astype(jnp.float32)).astype(jnp.bfloat16)
    return high, mid, low


def split2(value):
    high = value.astype(jnp.bfloat16)
    return high, (value - high.astype(jnp.float32)).astype(jnp.bfloat16)


def solve_rows(row, prior_row):
    entry = {}
    for index, (i, j) in enumerate(PAIR_LIST):
        entry[j, i] = row(index)
    for i in range(5):
        entry[i, i] = entry[i, i] + prior_row(i)
    right = [row(15 + i) for i in range(5)]
    unit, inverse = {}, []
    for col in range(5):
        inv = 1.0 / entry[col, col]
        inverse.append(inv)
        for r in range(col + 1, 5):
            unit[r, col] = entry[r, col] * inv
        for r in range(col + 1, 5):
            for c in range(col + 1, r + 1):
                entry[r, c] = entry[r, c] - unit[r, col] * entry[c, col]
            right[r] = right[r] - unit[r, col] * right[col]
    result = [right[i] * inverse[i] for i in range(5)]
    for i in range(4, 0, -1):
        for k in range(i):
            result[k] = result[k] - unit[i, k] * result[i]
    return result


def near_peers(tm, n_tm):
    if n_tm % 2 == 0 and n_tm <= 8:
        edges = [(tm + 1 - 2 * (tm % 2), None), (tm + 2, tm + 2 < n_tm), (tm - 2, tm >= 2)]
        return edges, n_tm // 2 - 1
    if n_tm & (n_tm - 1) == 0:
        bits = [1 << i for i in range(n_tm.bit_length() - 1)]
        return [(tm + bit * (1 - 2 * ((tm // bit) % 2)), None) for bit in bits], len(bits) - 1
    return [(lax.rem(tm + d, n_tm), None) for d in range(1, n_tm)], 0


def tell(semaphore, edges):
    for peer, exists in edges:

        def send(peer=peer):
            pl.semaphore_signal(semaphore, inc=1, device_id={"tm": peer}, device_id_type=MESH)

        if exists is None:
            send()
        else:
            pl.when(exists)(send)


def kernel(
    n_sky, n_tm, span,
    attitude_hbm, time_hbm, parallax_hbm, observed_hbm, phase_hbm, knot_hbm,
    source_hbm, count_hbm, prior_hbm,
    out_ref, prior_ref,
    table, coef, reals, ints, spread, parts, member, tiles, landed,
    real_sem, int_sem, prior_sem, own_sem, att_send, att_recv, sum_send, sum_recv, met,
):
    sky = lax.axis_index("sky")
    tm = lax.axis_index("tm")
    rows = time_hbm.shape[0]
    owned = tiles.shape[1]
    wide = source_hbm.shape[0]
    phase_v, time_v, parallax_v, observed_v = (reals.at[i] for i in range(4))
    knot_v = ints.at[:rows]
    source_v = ints.at[rows : rows + wide]
    count_v = ints.at[rows + wide :]
    sources = owned * n_tm
    segs = LANES // span

    barrier = pltpu.get_barrier_semaphore()
    for d in range(1, n_sky):
        pl.semaphore_signal(
            barrier, inc=1, device_id={"sky": lax.rem(sky + d, n_sky)}, device_id_type=MESH
        )
    edges, rounds = near_peers(tm, n_tm)
    degree = sum(1 if exists is None else exists.astype(jnp.int32) for _, exists in edges)
    tell(barrier, edges)
    own = pltpu.make_async_copy(attitude_hbm, table.at[sky], own_sem)
    own.start()
    for src, dst in ((source_hbm, source_v), (count_hbm, count_v), (knot_hbm, knot_v)):
        pltpu.make_async_copy(src, dst, int_sem).start()
    for i, src in enumerate((phase_hbm, time_hbm, parallax_hbm, observed_hbm)):
        pltpu.make_async_copy(src, reals.at[i], real_sem).start()
    prior_copy = pltpu.make_async_copy(prior_hbm, prior_ref, prior_sem)
    prior_copy.start()

    lane_out = lax.broadcasted_iota(jnp.int32, (LANES, LANES), 1)
    lane_in = lax.broadcasted_iota(jnp.int32, (LANES, LANES), 0)
    base = lane_out - (lane_in // span) * ROWS
    for x in range(20):
        spread[x * LANES : (x + 1) * LANES, :] = jnp.where(base == x, 1.0, 0.0).astype(jnp.bfloat16)

    own.wait()
    pl.semaphore_wait(barrier, n_sky - 1 + degree)

    for d in range(1, n_sky):
        pltpu.make_async_remote_copy(
            src_ref=table.at[sky],
            dst_ref=table.at[sky],
            send_sem=att_send,
            recv_sem=att_recv,
            device_id={"sky": lax.rem(sky + d, n_sky)},
            device_id_type=MESH,
        ).start()

    if rounds:
        tell(met.at[0], edges)
    pltpu.make_async_copy(ints, ints, int_sem).wait()

    width = 3 * rows
    lane = lax.broadcasted_iota(jnp.int32, (8, LANES), 1)
    sub = lax.broadcasted_iota(jnp.int32, (8, LANES), 0)
    id_list = []
    for start in range(0, width, LANES):
        block = ((lane + start) % rows) * segs + sub % segs
        got = lane_gather(source_v[0:1, :], block % LANES)
        for c in range(1, source_v.shape[0]):
            got = jnp.where(block // LANES == c, lane_gather(source_v[c : c + 1, :], block % LANES), got)
        id_list.append(got)
    ids = jnp.concatenate(id_list, axis=1)[:, :width]
    which = lax.broadcasted_iota(jnp.int32, (sources, width), 0)
    for q in range(segs):
        hit = jnp.broadcast_to(ids[q : q + 1, :], (sources, width)) == which
        member[q * sources : (q + 1) * sources, :] = jnp.where(hit, 1.0, 0.0).astype(jnp.bfloat16)

    for step in range(1, min(2, rounds)):
        pl.semaphore_wait(met.at[step - 1], degree)
        tell(met.at[step], edges)
    pltpu.make_async_copy(reals, reals, real_sem).wait()
    others = table.at[: n_sky - 1]
    pltpu.make_async_copy(others, others, att_recv).wait()

    for step in range(2, rounds):
        pl.semaphore_wait(met.at[step - 1], degree)
        tell(met.at[step], edges)

    per = table.shape[2] // LANES
    chunks = [
        table[c // per, :, (c % per) * LANES : (c % per + 1) * LANES] for c in range(n_sky * per)
    ]
    n_chunks = len(chunks)
    here = jnp.concatenate(chunks, axis=0)
    after = jnp.concatenate(chunks[1:] + chunks[-1:], axis=0)
    wide_lane = lax.broadcasted_iota(jnp.int32, here.shape, 1)
    a = [here]
    for i in range(1, 4):
        a.append(
            jnp.where(
                wide_lane < LANES - i,
                pltpu.roll(here, LANES - i, 1),
                pltpu.roll(after, LANES - i, 1),
            )
        )
    coef[0] = (a[0] + 4.0 * a[1] + a[2]) * (1.0 / 6.0)
    coef[1] = (a[2] - a[0]) * 0.5
    coef[2] = (a[0] - 2.0 * a[1] + a[2]) * 0.5
    coef[3] = ((a[3] - a[0]) + 3.0 * (a[1] - a[2])) * (1.0 / 6.0)

    def sums_of(v):
        at = slice(v * 8, v * 8 + 8)
        knot = knot_v[at, :]
        u = phase_v[at, :]
        time = time_v[at, :]
        block = (sub + v * 8) * segs + lane // span
        chunk = (v * 8 * segs) // LANES
        count = lane_gather(count_v[chunk : chunk + 1, :], block - chunk * LANES)
        live = lane % span < count
        low, high = knot % LANES, knot // LANES
        picks = [high == c for c in range(n_chunks)]
        quat = []
        for m in range(4):
            value = None
            for j in (3, 2, 1, 0):
                got = lane_gather(coef[j, m : m + 1, :], low)
                for c in range(1, n_chunks):
                    x = c * 4 + m
                    got = jnp.where(picks[c], lane_gather(coef[j, x : x + 1, :], low), got)
                value = got if value is None else value * u + got
            quat.append(value)
        q0, q1, q2, q3 = quat
        cross = jnp.where(live, q0 * q0 + q1 * q1 - q2 * q2 - q3 * q3, 0.0)
        along = jnp.where(live, 2.0 * (q1 * q2 + q0 * q3), 0.0)
        tilt = 2.0 * (q1 * q3 - q0 * q2)
        parallax = jnp.where(live, parallax_v[at, :], 0.0)
        design = [cross, along, parallax, time * cross, time * along]
        residual = observed_v[at, :] - tilt
        return [design[i] * design[j] for i, j in PAIR_LIST] + [d * residual for d in design]

    for v in range(0, rows // 8, 2):
        first, second = sums_of(v), sums_of(v + 1)
        for x in range(20):
            for k, part in enumerate(split2(jnp.concatenate([first[x], second[x]], axis=0))):
                parts[k * rows + v * 8 : k * rows + v * 8 + 16, x * LANES : (x + 1) * LANES] = part

    two = jnp.dot(parts[...], spread[...], preferred_element_type=jnp.float32)
    block_sum = two[:rows] + two[rows:]
    stacked = jnp.concatenate(split3(block_sum), axis=0)
    by_seg = jnp.dot(member[...], stacked, preferred_element_type=jnp.float32)
    lane_s = lax.broadcasted_iota(jnp.int32, (sources, LANES), 1) // ROWS
    normal = jnp.where(lane_s == 0, by_seg[:sources], 0.0)
    for q in range(1, segs):
        normal = jnp.where(lane_s == q, by_seg[q * sources : (q + 1) * sources], normal)
    tiles[...] = normal.reshape(n_tm, owned, LANES)
    if rounds:
        pl.semaphore_wait(met.at[rounds - 1], degree)

    for d in range(1, n_tm):
        peer = lax.rem(tm + d, n_tm)
        pltpu.make_async_remote_copy(
            src_ref=tiles.at[peer],
            dst_ref=landed.at[d - 1],
            send_sem=sum_send,
            recv_sem=sum_recv,
            device_id={"tm": peer},
            device_id_type=MESH,
        ).start()
    total = tiles[tm]
    pltpu.make_async_copy(landed, landed, sum_recv).wait()
    for d in range(1, n_tm):
        total = total + landed[d - 1]
    out_ref[...] = total
    prior_copy.wait()
    pltpu.make_async_copy(others, others, att_send).wait()
    pltpu.make_async_copy(landed, landed, sum_send).wait()


def solve_kernel(total_ref, prior_ref, out_ref, turned):
    total = total_ref[...]
    full = total
    for shift in range(ROWS, LANES, ROWS):
        full = full + pltpu.roll(total, shift, 1)
    turned[...] = jnp.transpose(full)
    result = solve_rows(lambda i: turned[i : i + 1, :], lambda i: prior_ref[i : i + 1, :])
    for i in range(5):
        out_ref[i : i + 1, :] = result[i]


def on_device(n_sky, n_tm, attitude, time, parallax, observed, phase, knot, source, count, prior):
    slots, blocks, owned = time.shape[0], source.shape[0], prior.shape[1]
    knots = attitude.shape[2]
    rows = slots // LANES
    span = slots // blocks
    sources = owned * n_tm
    segs = LANES // span
    n_chunks = n_sky * knots // LANES
    shape = (rows, LANES)
    vmem = pltpu.VMEM
    f32, i32, bf16 = jnp.float32, jnp.int32, jnp.bfloat16
    total, prior_near = pl.pallas_call(
        functools.partial(kernel, n_sky, n_tm, span),
        out_shape=(pltpu.VMEM((owned, LANES), f32), pltpu.VMEM(prior.shape, f32)),
        in_specs=[pl.BlockSpec(memory_space=pl.ANY)] * 9,
        out_specs=(pl.BlockSpec(memory_space=pltpu.VMEM),) * 2,
        scratch_shapes=[
            vmem((n_sky, 4, knots), f32),
            vmem((4, n_chunks * 4, LANES), f32),
            vmem((4,) + shape, f32),
            vmem((rows + 2 * (blocks // LANES), LANES), i32),
            vmem((20 * LANES, LANES), bf16),
            vmem((2 * rows, 20 * LANES), bf16),
            vmem((segs * sources, 3 * rows), bf16),
            vmem((n_tm, owned, LANES), f32),
            vmem((n_tm - 1, owned, LANES), f32),
        ]
        + [pltpu.SemaphoreType.DMA] * 8
        + [pltpu.SemaphoreType.REGULAR((max(1, near_peers(0, n_tm)[1]),))],
        compiler_params=pltpu.CompilerParams(collective_id=0, has_side_effects=True),
    )(
        attitude.reshape(4, knots),
        time.reshape(shape),
        parallax.reshape(shape),
        observed.reshape(shape),
        phase.reshape(shape),
        knot.reshape(shape),
        source.reshape(blocks // LANES, LANES),
        count.reshape(blocks // LANES, LANES),
        prior,
    )
    return pl.pallas_call(
        solve_kernel,
        out_shape=jax.ShapeDtypeStruct(prior.shape, f32),
        in_specs=[pl.BlockSpec(memory_space=pltpu.VMEM)] * 2,
        scratch_shapes=[vmem((LANES, owned), f32)],
    )(
        pltpu.with_memory_space_constraint(total, pltpu.VMEM),
        pltpu.with_memory_space_constraint(prior_near, pltpu.VMEM),
    )


def solution(mesh):
    slot = P(("sky", "tm"))
    in_specs = (P(None, "tm", "sky"),) + (slot,) * 7 + (P(None, ("sky", "tm")),)
    return jax.shard_map(
        functools.partial(on_device, mesh.shape["sky"], mesh.shape["tm"]),
        mesh=mesh,
        in_specs=in_specs,
        out_specs=P(None, ("sky", "tm")),
        check_vma=False,
    )
```

profile of v0, /device:TPU:0, one launch (start us, length us, event | category | flops | bytes accessed | tf_op | source)
XLA Modules:
  0.0 13.8 jit_solution(18308055473653686817)
XLA Ops:
  0.0 13.0 %shard_map.91 = (f32[8,128]{1,0:T(8,128)S(1)}, f32[5,8]{1,0:T(8,128)S(1)}) custom-call(f32[4,128]{1,0:T(4,128)} %bitcast.13, f32[64,128]{1,0:T(8,128)} %bitcast.8, f32[64,128]{1,0:T(8,128)} %bitcast.9, f32[64,128]{1,0:T(8,128)} %bitcast.10, f32[64,128]{1,0:T(8,128)} %bitcast.11, s32[64,128]{1,0:T(8,128)} %bitcast.12, s32[2,128]{1,0:T(2,128)} %bitcast.14, ...), custom_call_target="tpu_custom_call" | custom-call | tf_op jit(solution)/shard_map/pallas_call | solution.py:279
  13.0 0.8 %shard_map.92 = f32[5,8]{1,0:T(8,128)} custom-call(f32[8,128]{1,0:T(8,128)S(1)} %get-tuple-element.7.total_ref, f32[5,8]{1,0:T(8,128)S(1)} %get-tuple-element.8.prior_ref), custom_call_target="tpu_custom_call" | custom-call | tf_op jit(solution)/shard_map/pallas_call | solution.py:309
where the time goes:
time: 14 us; the launch traced here: 13.8 us
  Pallas kernels  13.8 us (99%)
    pallas_call x1, Pallas kernels, on_device(): pl.pallas_call(functools.partial(kernel, n_sky, n_tm, span), out_shape=(p...  13 us
    pallas_call x1, Pallas kernels, on_device(): pl.pallas_call(solve_kernel, out_shape=jax.ShapeDtypeStruct(prior.shape,...  0.79 us

commit v1 on v0

v1 whole, which is shorter than its diff:
```python
import functools

import jax
import jax.numpy as jnp
from jax import lax
from jax.experimental import pallas as pl
from jax.experimental.pallas import tpu as pltpu
from jax.sharding import PartitionSpec as P

PAIR_LIST = [(i, j) for i in range(5) for j in range(i, 5)]
MESH = pl.DeviceIdType.MESH
LANES = 128
SUBS = 8
ROWS = 32


def lane_gather(row, index):
    wide = jnp.broadcast_to(row, index.shape)
    return jnp.take_along_axis(wide, index, axis=1, mode="promise_in_bounds")


def split2(value):
    high = value.astype(jnp.bfloat16)
    return high, (value - high.astype(jnp.float32)).astype(jnp.bfloat16)


def solve_rows(row, prior_row):
    entry = {}
    for i, j in PAIR_LIST:
        entry[j, i] = row(PLACE[i, j])
    for i in range(5):
        entry[i, i] = entry[i, i] + prior_row(i)
    right = [row(PLACE[i]) for i in range(5)]
    unit, inverse = {}, []
    for col in range(5):
        inv = 1.0 / entry[col, col]
        inverse.append(inv)
        for r in range(col + 1, 5):
            unit[r, col] = entry[r, col] * inv
        for r in range(col + 1, 5):
            for c in range(col + 1, r + 1):
                entry[r, c] = entry[r, c] - unit[r, col] * entry[c, col]
            right[r] = right[r] - unit[r, col] * right[col]
    result = [right[i] * inverse[i] for i in range(5)]
    for i in range(4, 0, -1):
        for k in range(i):
            result[k] = result[k] - unit[i, k] * result[i]
    return result


PLACE = {
    (0, 0): 0, (0, 1): 1, (0, 3): 2, (0, 4): 3, (1, 3): 3, (1, 1): 4, (1, 4): 5, (3, 3): 6, (3, 4): 7,
    (4, 4): 8, (0, 2): 9, (1, 2): 10, (2, 3): 11, (2, 4): 12, 0: 13, 1: 14, 2: 15,
    3: 16, 4: 17, (2, 2): 18,
}
SUMS = 19


def near_peers(tm, n_tm):
    if n_tm % 2 == 0 and n_tm <= 8:
        edges = [(tm + 1 - 2 * (tm % 2), None), (tm + 2, tm + 2 < n_tm), (tm - 2, tm >= 2)]
        return edges, n_tm // 2 - 1
    if n_tm & (n_tm - 1) == 0:
        bits = [1 << i for i in range(n_tm.bit_length() - 1)]
        return [(tm + bit * (1 - 2 * ((tm // bit) % 2)), None) for bit in bits], len(bits) - 1
    return [(lax.rem(tm + d, n_tm), None) for d in range(1, n_tm)], 0


def sky_peers(sky, n_sky):
    if n_sky & (n_sky - 1):
        sends = [(lax.rem(sky + d, n_sky), d) for d in range(1, n_sky)]
        return sends, [(lax.rem(sky + n_sky - d, n_sky), d) for d in range(1, n_sky)]
    core = sky % 2
    mate = sky + 1 - 2 * core
    sends, arrivals = [(mate, core)], [(mate, 1 - core)]
    for k in range(1, n_sky // 2):
        base = sky - core
        for bit in [1 << i for i in range(1, n_sky.bit_length())]:
            if 2 * k & bit:
                base = base + bit * (1 - 2 * ((sky // bit) % 2))
        sends += [(base, 2 * k + core), (base + 1, 2 * k + core)]
        arrivals += [(base + 1, 2 * k + 1), (base, 2 * k)]
    return sends, arrivals


def tell(semaphore, edges):
    for peer, exists in edges:

        def send(peer=peer):
            pl.semaphore_signal(semaphore, inc=1, device_id={"tm": peer}, device_id_type=MESH)

        if exists is None:
            send()
        else:
            pl.when(exists)(send)


def fold_subs(values, sub):
    values = list(values) + [jnp.zeros_like(values[0])] * (SUBS - len(values))
    values = [values[i] for i in (0, 4, 2, 6, 1, 5, 3, 7)]
    step = 1
    while step < SUBS:
        low = (sub // step) % 2 == 0
        half = len(values) // 2
        values = [
            jnp.where(low, a, b) + pltpu.roll(jnp.where(low, b, a), step, 0)
            for a, b in zip(values[:half], values[half:])
        ]
        step *= 2
    return values[0]


def kernel(
    n_sky, n_tm, span,
    attitude_hbm, time_hbm, parallax_hbm, observed_hbm, phase_hbm, knot_hbm,
    source_hbm, count_hbm, prior_hbm,
    out_ref, prior_ref,
    table, reals, ints, low, high, weight, masked, fact, quat, square, member, tiles, landed,
    real_sem, int_sem, prior_sem, own_sem, att_send, att_recv, sum_send, sum_recv, met,
):
    sky = lax.axis_index("sky")
    tm = lax.axis_index("tm")
    rows = time_hbm.shape[0]
    owned = tiles.shape[1]
    wide = source_hbm.shape[0]
    phase_v, time_v, parallax_v, observed_v = (reals.at[i] for i in range(4))
    knot_v = ints.at[:rows]
    source_v = ints.at[rows : rows + wide]
    count_v = ints.at[rows + wide :]
    sources = owned * n_tm
    segs = LANES // span
    fold = LANES // rows
    halves = segs // fold
    steps = span // SUBS

    own = pltpu.make_async_copy(attitude_hbm, table.at[sky], own_sem)
    own.start()
    barrier = pltpu.get_barrier_semaphore()
    sends, arrivals = sky_peers(sky, n_sky)
    for peer, _ in sends:
        pl.semaphore_signal(barrier, inc=1, device_id={"sky": peer}, device_id_type=MESH)
    edges, rounds = near_peers(tm, n_tm)
    degree = sum(1 if exists is None else exists.astype(jnp.int32) for _, exists in edges)
    tell(barrier, edges)
    for src, dst in ((source_hbm, source_v), (count_hbm, count_v), (knot_hbm, knot_v)):
        pltpu.make_async_copy(src, dst, int_sem).start()
    for i, src in enumerate((phase_hbm, time_hbm, parallax_hbm, observed_hbm)):
        pltpu.make_async_copy(src, reals.at[i], real_sem).start()
    prior_copy = pltpu.make_async_copy(prior_hbm, prior_ref, prior_sem)
    prior_copy.start()

    tiles[...] = jnp.zeros_like(tiles)

    own.wait()
    pl.semaphore_wait(barrier, n_sky - 1 + degree)
    for peer, there in sends:
        pltpu.make_async_remote_copy(
            src_ref=table.at[sky],
            dst_ref=table.at[sky],
            send_sem=att_send,
            recv_sem=att_recv.at[there],
            device_id={"sky": peer},
            device_id_type=MESH,
        ).start()
    if rounds:
        tell(met.at[0], edges)

    pltpu.make_async_copy(ints, ints, int_sem).wait()
    lane = lax.broadcasted_iota(jnp.int32, (SUBS, LANES), 1)
    sub = lax.broadcasted_iota(jnp.int32, (SUBS, LANES), 0)
    count = []
    which = lax.broadcasted_iota(jnp.int32, (sources, LANES), 0)
    for h in range(halves):
        block = (lane % rows) * segs + h * fold + lane // rows

        def of_block(ref):
            got = lane_gather(ref[0:1, :], block % LANES)
            for c in range(1, wide):
                got = jnp.where(block // LANES == c, lane_gather(ref[c : c + 1, :], block % LANES), got)
            return got

        count.append(of_block(count_v))
        hit = jnp.broadcast_to(of_block(source_v)[0:1, :], (sources, LANES)) == which
        one = jnp.where(hit, 1.0, 0.0).astype(jnp.bfloat16)
        for k in range(2):
            at = (k * halves + h) * LANES
            member[:, at : at + LANES] = one

    def turn(value):
        parts = [value] + [pltpu.roll(value, LANES - e * span, 1) for e in range(1, fold)]
        turned = jnp.transpose(jnp.concatenate(parts, axis=0))
        return [turned[h * fold * span : h * fold * span + span, :] for h in range(halves)]

    for h, knot in enumerate(turn(knot_v[...])):
        at = slice(h * span, h * span + span)
        low[at, :] = knot % LANES
        high[at, :] = knot // LANES

    pltpu.make_async_copy(reals, reals, real_sem).wait()
    turned = [turn(ref[...]) for ref in (phase_v, time_v, parallax_v, observed_v)]
    for h in range(halves):
        at = slice(h * span, h * span + span)
        u, time, parallax, observed = (t[h] for t in turned)
        slot = lax.broadcasted_iota(jnp.int32, (span, LANES), 0)
        live = slot < jnp.broadcast_to(count[h][0:1, :], (span, LANES))
        u2, v = u * u, 1.0 - u
        u3 = u2 * u
        spline = (
            v * v * v * (1.0 / 6.0),
            0.5 * u3 - u2 + (2.0 / 3.0),
            0.5 * (u + u2 - u3) + (1.0 / 6.0),
            u3 * (1.0 / 6.0),
        )
        for i in range(4):
            weight[i, at, :] = jnp.where(live, spline[i], 0.0)
        parallax = jnp.where(live, parallax, 0.0)
        fact[0, at, :] = time
        fact[1, at, :] = time * time
        fact[2, at, :] = parallax
        fact[3, at, :] = parallax * time
        fact[4, at, :] = observed
        both = parallax * parallax
        total = both[:SUBS]
        for g in range(1, steps):
            total = total + both[g * SUBS : (g + 1) * SUBS]
        square[h] = total

    if rounds:
        pl.semaphore_wait(met.at[0], degree)
        if rounds > 1:
            tell(met.at[1], edges)

    per = table.shape[2] // LANES

    def mask_weights(chunk):
        lows, highs = low[...], high[...]
        for i in range(4):
            there = highs + (lows >= LANES - i).astype(jnp.int32) if i else highs
            masked[i] = jnp.where(there == chunk, weight[i], 0.0)

    def rows_of(source, p):
        here = table[source, :, p * LANES : (p + 1) * LANES]
        return [here] + [pltpu.roll(here, LANES - i, 1) for i in range(1, 4)]

    def gather(shifted, v, carry):
        at = slice(v * SUBS, v * SUBS + SUBS)
        index = low[at, :]
        scale = [masked[i, at, :] for i in range(4)]
        got = []
        for m in range(4):
            value = carry[m] if carry else None
            for i in range(4):
                term = lane_gather(shifted[i][m : m + 1, :], index) * scale[i]
                value = term if value is None else value + term
            got.append(value)
        return got

    pieces = [(sky, None, p) for p in range(per)]
    for source, here in arrivals:
        pieces += [(source, here if p == 0 else None, p) for p in range(per)]
    for n, (source, here, p) in enumerate(pieces):
        mask_weights(source * per + p)
        if n == 1:
            for step in range(2, rounds):
                pl.semaphore_wait(met.at[step - 1], degree)
                tell(met.at[step], edges)
        if here is not None:
            arrived = table.at[source]
            pltpu.make_async_copy(arrived, arrived, att_recv.at[here]).wait()
        shifted = rows_of(source, p)
        if n + 1 < len(pieces):
            for v in range(rows // SUBS):
                at = slice(v * SUBS, v * SUBS + SUBS)
                got = gather(shifted, v, [quat[m, at, :] for m in range(4)] if n else None)
                for m in range(4):
                    quat[m, at, :] = got[m]

    stacked = []
    for h in range(halves):
        sums = None
        for g in range(steps):
            v = h * steps + g
            at = slice(v * SUBS, v * SUBS + SUBS)
            carry = [quat[m, at, :] for m in range(4)] if len(pieces) > 1 else None
            q0, q1, q2, q3 = gather(shifted, v, carry)
            cross = (q0 * q0 + q1 * q1) - (q2 * q2 + q3 * q3)
            along = 2.0 * (q1 * q2 + q0 * q3)
            tilt = 2.0 * (q1 * q3 - q0 * q2)
            t, tt, p, tp, o = (fact[i, at, :] for i in range(5))
            rest = o - tilt
            cc, ca, aa = cross * cross, cross * along, along * along
            cr, ar = cross * rest, along * rest
            new = {
                (0, 0): cc, (0, 1): ca, (0, 3): t * cc, (0, 4): t * ca, (1, 1): aa, (1, 4): t * aa,
                (3, 3): tt * cc, (3, 4): tt * ca, (4, 4): tt * aa,
                (0, 2): p * cross, (1, 2): p * along, (2, 3): tp * cross, (2, 4): tp * along,
                0: cr, 1: ar, 2: p * rest, 3: t * cr, 4: t * ar,
            }
            sums = new if sums is None else {key: sums[key] + new[key] for key in new}
        sums[2, 2] = square[h]
        line = [sums[key] for key in sorted(sums, key=lambda key: PLACE[key])]
        groups = [fold_subs(line[i : i + SUBS], sub) for i in range(0, SUMS, SUBS)]
        groups += [jnp.zeros_like(groups[0])] * (ROWS // SUBS - len(groups))
        stacked.append(jnp.concatenate(groups, axis=0))
    split = [split2(value) for value in stacked]
    packed = jnp.concatenate([s[k] for k in range(2) for s in split], axis=1)
    normal = lax.dot_general(
        member[...], packed, (((1,), (1,)), ((), ())), preferred_element_type=jnp.float32
    )
    tiles[:, :, :ROWS] = normal.reshape(n_tm, owned, ROWS)
    if rounds:
        pl.semaphore_wait(met.at[rounds - 1], degree)

    for d in range(1, n_tm):
        peer = lax.rem(tm + d, n_tm)
        pltpu.make_async_remote_copy(
            src_ref=tiles.at[peer],
            dst_ref=landed.at[d - 1],
            send_sem=sum_send,
            recv_sem=sum_recv,
            device_id={"tm": peer},
            device_id_type=MESH,
        ).start()
    prior_copy.wait()
    others = table.at[: n_sky - 1]
    pltpu.make_async_copy(others, others, att_send).wait()
    total = tiles[tm]
    pltpu.make_async_copy(landed, landed, sum_recv).wait()
    for d in range(1, n_tm):
        total = total + landed[d - 1]
    out_ref[...] = total
    pltpu.make_async_copy(landed, landed, sum_send).wait()


def solve_kernel(total_ref, prior_ref, out_ref, turned):
    turned[...] = jnp.transpose(total_ref[...])[:ROWS]
    result = solve_rows(lambda i: turned[i : i + 1, :], lambda i: prior_ref[i : i + 1, :])
    for i in range(5):
        out_ref[i : i + 1, :] = result[i]


def on_device(n_sky, n_tm, attitude, time, parallax, observed, phase, knot, source, count, prior):
    slots, blocks, owned = time.shape[0], source.shape[0], prior.shape[1]
    knots = attitude.shape[2]
    rows = slots // LANES
    span = slots // blocks
    sources = owned * n_tm
    shape = (rows, LANES)
    vmem = pltpu.VMEM
    f32, i32, bf16 = jnp.float32, jnp.int32, jnp.bfloat16
    halves = (LANES // span) // (LANES // rows)
    total, prior_near = pl.pallas_call(
        functools.partial(kernel, n_sky, n_tm, span),
        out_shape=(pltpu.VMEM((owned, LANES), f32), pltpu.VMEM(prior.shape, f32)),
        in_specs=[pl.BlockSpec(memory_space=pl.ANY)] * 9,
        out_specs=(pl.BlockSpec(memory_space=pltpu.VMEM),) * 2,
        scratch_shapes=[
            vmem((n_sky, 4, knots), f32),
            vmem((4,) + shape, f32),
            vmem((rows + 2 * (blocks // LANES), LANES), i32),
            vmem(shape, i32),
            vmem(shape, i32),
            vmem((4,) + shape, f32),
            vmem((4,) + shape, f32),
            vmem((5,) + shape, f32),
            vmem((4,) + shape, f32),
            vmem((halves, SUBS, LANES), f32),
            vmem((sources, 2 * blocks), bf16),
            vmem((n_tm, owned, LANES), f32),
            vmem((n_tm - 1, owned, LANES), f32),
        ]
        + [pltpu.SemaphoreType.DMA] * 5
        + [pltpu.SemaphoreType.DMA((n_sky,))]
        + [pltpu.SemaphoreType.DMA] * 2
        + [pltpu.SemaphoreType.REGULAR((max(1, near_peers(0, n_tm)[1]),))],
        compiler_params=pltpu.CompilerParams(collective_id=0, has_side_effects=True),
    )(
        attitude.reshape(4, knots),
        time.reshape(shape),
        parallax.reshape(shape),
        observed.reshape(shape),
        phase.reshape(shape),
        knot.reshape(shape),
        source.reshape(blocks // LANES, LANES),
        count.reshape(blocks // LANES, LANES),
        prior,
    )
    return pl.pallas_call(
        solve_kernel,
        out_shape=jax.ShapeDtypeStruct(prior.shape, f32),
        in_specs=[pl.BlockSpec(memory_space=pltpu.VMEM)] * 2,
        scratch_shapes=[vmem((ROWS, owned), f32)],
    )(
        pltpu.with_memory_space_constraint(total, pltpu.VMEM),
        pltpu.with_memory_space_constraint(prior_near, pltpu.VMEM),
    )


def solution(mesh):
    slot = P(("sky", "tm"))
    in_specs = (P(None, "tm", "sky"),) + (slot,) * 7 + (P(None, ("sky", "tm")),)
    return jax.shard_map(
        functools.partial(on_device, mesh.shape["sky"], mesh.shape["tm"]),
        mesh=mesh,
        in_specs=in_specs,
        out_specs=P(None, ("sky", "tm")),
        check_vma=False,
    )
```

time: 14 us -> 13.2 us (0.943)
  Pallas kernels: 13.8 us -> 13.1 us
    pallas_call x1, Pallas kernels: 13 us -> 12.3 us  [on_device(): pl.pallas_call(functools.partial(kernel, n_sky, n_tm, span), out_shape=(p...]
where the time goes in v1:
time: 13.2 us; the launch traced here: 13.1 us
  Pallas kernels  13.1 us (99%)
    pallas_call x1, Pallas kernels, on_device(): pl.pallas_call(functools.partial(kernel, n_sky, n_tm, span), out_shape=(p...  12.3 us
    pallas_call x1, Pallas kernels, on_device(): pl.pallas_call(solve_kernel, out_shape=jax.ShapeDtypeStruct(prior.shape,...  0.72 us

profile of v1, /device:TPU:0, one launch (start us, length us, event | category | flops | bytes accessed | tf_op | source)
XLA Modules:
  0.0 13.1 jit_solution(6152252429710782300)
XLA Ops:
  0.0 12.3 %shard_map.91 = (f32[8,128]{1,0:T(8,128)S(1)}, f32[5,8]{1,0:T(8,128)S(1)}) custom-call(f32[4,128]{1,0:T(4,128)} %bitcast.13, f32[64,128]{1,0:T(8,128)} %bitcast.8, f32[64,128]{1,0:T(8,128)} %bitcast.9, f32[64,128]{1,0:T(8,128)} %bitcast.10, f32[64,128]{1,0:T(8,128)} %bitcast.11, s32[64,128]{1,0:T(8,128)} %bitcast.12, s32[2,128]{1,0:T(2,128)} %bitcast.14, ...), custom_call_target="tpu_custom_call" | custom-call | tf_op jit(solution)/shard_map/pallas_call | solution.py:352
  12.4 0.7 %shard_map.92 = f32[5,8]{1,0:T(8,128)} custom-call(f32[8,128]{1,0:T(8,128)S(1)} %get-tuple-element.7.total_ref, f32[5,8]{1,0:T(8,128)S(1)} %get-tuple-element.8.prior_ref), custom_call_target="tpu_custom_call" | custom-call | tf_op jit(solution)/shard_map/pallas_call | solution.py:388

commit v2 on v1

--- a/solution.py
+++ b/solution.py
@@ -56,14 +56,8 @@
 SUMS = 19
 
 
-def near_peers(tm, n_tm):
-    if n_tm % 2 == 0 and n_tm <= 8:
-        edges = [(tm + 1 - 2 * (tm % 2), None), (tm + 2, tm + 2 < n_tm), (tm - 2, tm >= 2)]
-        return edges, n_tm // 2 - 1
-    if n_tm & (n_tm - 1) == 0:
-        bits = [1 << i for i in range(n_tm.bit_length() - 1)]
-        return [(tm + bit * (1 - 2 * ((tm // bit) % 2)), None) for bit in bits], len(bits) - 1
-    return [(lax.rem(tm + d, n_tm), None) for d in range(1, n_tm)], 0
+def rank_of(tm, n_tm):
+    return tm // 2 + tm % 2 if n_tm % 2 == 0 and n_tm <= 8 else tm
 
 
 def sky_peers(sky, n_sky):
@@ -83,16 +77,10 @@
     return sends, arrivals
 
 
-def tell(semaphore, edges):
-    for peer, exists in edges:
-
-        def send(peer=peer):
-            pl.semaphore_signal(semaphore, inc=1, device_id={"tm": peer}, device_id_type=MESH)
-
-        if exists is None:
-            send()
-        else:
-            pl.when(exists)(send)
+def tell(semaphore, peer, exists):
+    @pl.when(exists)
+    def _():
+        pl.semaphore_signal(semaphore, inc=1, device_id={"tm": peer}, device_id_type=MESH)
 
 
 def fold_subs(values, sub):
@@ -139,20 +127,23 @@
     sends, arrivals = sky_peers(sky, n_sky)
     for peer, _ in sends:
         pl.semaphore_signal(barrier, inc=1, device_id={"sky": peer}, device_id_type=MESH)
-    edges, rounds = near_peers(tm, n_tm)
-    degree = sum(1 if exists is None else exists.astype(jnp.int32) for _, exists in edges)
-    tell(barrier, edges)
     for src, dst in ((source_hbm, source_v), (count_hbm, count_v), (knot_hbm, knot_v)):
         pltpu.make_async_copy(src, dst, int_sem).start()
     for i, src in enumerate((phase_hbm, time_hbm, parallax_hbm, observed_hbm)):
         pltpu.make_async_copy(src, reals.at[i], real_sem).start()
     prior_copy = pltpu.make_async_copy(prior_hbm, prior_ref, prior_sem)
     prior_copy.start()
+    rank = rank_of(tm, n_tm)
+    ranks = [rank_of(peer, n_tm) for peer in range(n_tm)]
+    below = sum((rank > other).astype(jnp.int32) for other in ranks)
+    above = sum((rank < other).astype(jnp.int32) for other in ranks)
+    for peer, other in enumerate(ranks):
+        tell(barrier, peer, rank < other)
 
     tiles[...] = jnp.zeros_like(tiles)
 
     own.wait()
-    pl.semaphore_wait(barrier, n_sky - 1 + degree)
+    pl.semaphore_wait(barrier, n_sky - 1 + below)
     for peer, there in sends:
         pltpu.make_async_remote_copy(
             src_ref=table.at[sky],
@@ -162,8 +153,8 @@
             device_id={"sky": peer},
             device_id_type=MESH,
         ).start()
-    if rounds:
-        tell(met.at[0], edges)
+    for peer, other in enumerate(ranks):
+        tell(met, peer, rank > other)
 
     pltpu.make_async_copy(ints, ints, int_sem).wait()
     lane = lax.broadcasted_iota(jnp.int32, (SUBS, LANES), 1)
@@ -225,11 +216,6 @@
             total = total + both[g * SUBS : (g + 1) * SUBS]
         square[h] = total
 
-    if rounds:
-        pl.semaphore_wait(met.at[0], degree)
-        if rounds > 1:
-            tell(met.at[1], edges)
-
     per = table.shape[2] // LANES
 
     def mask_weights(chunk):
@@ -260,10 +246,6 @@
         pieces += [(source, here if p == 0 else None, p) for p in range(per)]
     for n, (source, here, p) in enumerate(pieces):
         mask_weights(source * per + p)
-        if n == 1:
-            for step in range(2, rounds):
-                pl.semaphore_wait(met.at[step - 1], degree)
-                tell(met.at[step], edges)
         if here is not None:
             arrived = table.at[source]
             pltpu.make_async_copy(arrived, arrived, att_recv.at[here]).wait()
@@ -308,8 +290,10 @@
         member[...], packed, (((1,), (1,)), ((), ())), preferred_element_type=jnp.float32
     )
     tiles[:, :, :ROWS] = normal.reshape(n_tm, owned, ROWS)
-    if rounds:
-        pl.semaphore_wait(met.at[rounds - 1], degree)
+
+    @pl.when(above > 0)
+    def _():
+        pl.semaphore_wait(met, above)
 
     for d in range(1, n_tm):
         peer = lax.rem(tm + d, n_tm)
@@ -372,7 +356,7 @@
         + [pltpu.SemaphoreType.DMA] * 5
         + [pltpu.SemaphoreType.DMA((n_sky,))]
         + [pltpu.SemaphoreType.DMA] * 2
-        + [pltpu.SemaphoreType.REGULAR((max(1, near_peers(0, n_tm)[1]),))],
+        + [pltpu.SemaphoreType.REGULAR],
         compiler_params=pltpu.CompilerParams(collective_id=0, has_side_effects=True),
     )(
         attitude.reshape(4, knots),

time: 13.2 us -> 12.9 us (0.977)
  Pallas kernels: 13.1 us -> 12.7 us
    pallas_call x1, Pallas kernels: 12.3 us -> 12 us  [on_device(): pl.pallas_call(functools.partial(kernel, n_sky, n_tm, span), out_shape=(p...]
where the time goes in v2:
time: 12.9 us; the launch traced here: 12.7 us
  Pallas kernels  12.7 us (98%)
    pallas_call x1, Pallas kernels, on_device(): pl.pallas_call(functools.partial(kernel, n_sky, n_tm, span), out_shape=(p...  12 us
    pallas_call x1, Pallas kernels, on_device(): pl.pallas_call(solve_kernel, out_shape=jax.ShapeDtypeStruct(prior.shape,...  0.72 us

profile of v2, /device:TPU:0, one launch (start us, length us, event | category | flops | bytes accessed | tf_op | source)
XLA Modules:
  0.0 12.7 jit_solution(17303851122993077456)
XLA Ops:
  0.0 12.0 %shard_map.91 = (f32[8,128]{1,0:T(8,128)S(1)}, f32[5,8]{1,0:T(8,128)S(1)}) custom-call(f32[4,128]{1,0:T(4,128)} %bitcast.13, f32[64,128]{1,0:T(8,128)} %bitcast.8, f32[64,128]{1,0:T(8,128)} %bitcast.9, f32[64,128]{1,0:T(8,128)} %bitcast.10, f32[64,128]{1,0:T(8,128)} %bitcast.11, s32[64,128]{1,0:T(8,128)} %bitcast.12, s32[2,128]{1,0:T(2,128)} %bitcast.14, ...), custom_call_target="tpu_custom_call" | custom-call | tf_op jit(solution)/shard_map/pallas_call | solution.py:336
  12.0 0.7 %shard_map.92 = f32[5,8]{1,0:T(8,128)} custom-call(f32[8,128]{1,0:T(8,128)S(1)} %get-tuple-element.7.total_ref, f32[5,8]{1,0:T(8,128)S(1)} %get-tuple-element.8.prior_ref), custom_call_target="tpu_custom_call" | custom-call | tf_op jit(solution)/shard_map/pallas_call | solution.py:372

commit v3 on v2

--- a/solution.py
+++ b/solution.py
@@ -56,25 +56,37 @@
 SUMS = 19
 
 
-def rank_of(tm, n_tm):
-    return tm // 2 + tm % 2 if n_tm % 2 == 0 and n_tm <= 8 else tm
+def orders(tm, n_tm):
+    if n_tm % 2 == 0 and n_tm <= 8:
+
+        def order(peer):
+            up, across = peer // 2, peer % 2
+            earlier = jnp.logical_and(tm // 2 >= up, tm % 2 >= across)
+            later = jnp.logical_and(tm // 2 <= up, tm % 2 <= across)
+            return jnp.logical_and(earlier, tm != peer), jnp.logical_and(later, tm != peer)
+    else:
+
+        def order(peer):
+            return tm > peer, tm < peer
+
+    return [(peer, *order(peer)) for peer in range(n_tm)]
 
 
 def sky_peers(sky, n_sky):
     if n_sky & (n_sky - 1):
-        sends = [(lax.rem(sky + d, n_sky), d) for d in range(1, n_sky)]
-        return sends, [(lax.rem(sky + n_sky - d, n_sky), d) for d in range(1, n_sky)]
+        sends = [(lax.rem(sky + d, n_sky), d - 1) for d in range(1, n_sky)]
+        return sends, [(lax.rem(sky + n_sky - d, n_sky), d - 1) for d in range(1, n_sky)]
     core = sky % 2
     mate = sky + 1 - 2 * core
-    sends, arrivals = [(mate, core)], [(mate, 1 - core)]
+    sends, arrivals = [], [(mate, 0)]
     for k in range(1, n_sky // 2):
         base = sky - core
         for bit in [1 << i for i in range(1, n_sky.bit_length())]:
             if 2 * k & bit:
                 base = base + bit * (1 - 2 * ((sky // bit) % 2))
-        sends += [(base, 2 * k + core), (base + 1, 2 * k + core)]
-        arrivals += [(base + 1, 2 * k + 1), (base, 2 * k)]
-    return sends, arrivals
+        sends += [(base, 2 * k - 1 + core), (base + 1, 2 * k - 1 + core)]
+        arrivals += [(base + 1, 2 * k), (base, 2 * k - 1)]
+    return sends + [(mate, 0)], arrivals
 
 
 def tell(semaphore, peer, exists):
@@ -102,10 +114,12 @@
     n_sky, n_tm, span,
     attitude_hbm, time_hbm, parallax_hbm, observed_hbm, phase_hbm, knot_hbm,
     source_hbm, count_hbm, prior_hbm,
-    out_ref, prior_ref,
-    table, reals, ints, low, high, weight, masked, fact, quat, square, member, tiles, landed,
-    real_sem, int_sem, prior_sem, own_sem, att_send, att_recv, sum_send, sum_recv, met,
+    out_ref,
+    mine, table, reals, ints, low, high, weight, masked, fact, quat, square, member, tiles, landed,
+    real_sem, int_sem, send_sem, att_recv, sum_recv, met, prior_ref, flat, packed,
 ):
+    own = pltpu.make_async_copy(attitude_hbm, mine, send_sem)
+    own.start()
     sky = lax.axis_index("sky")
     tm = lax.axis_index("tm")
     rows = time_hbm.shape[0]
@@ -121,8 +135,6 @@
     halves = segs // fold
     steps = span // SUBS
 
-    own = pltpu.make_async_copy(attitude_hbm, table.at[sky], own_sem)
-    own.start()
     barrier = pltpu.get_barrier_semaphore()
     sends, arrivals = sky_peers(sky, n_sky)
     for peer, _ in sends:
@@ -131,14 +143,11 @@
         pltpu.make_async_copy(src, dst, int_sem).start()
     for i, src in enumerate((phase_hbm, time_hbm, parallax_hbm, observed_hbm)):
         pltpu.make_async_copy(src, reals.at[i], real_sem).start()
-    prior_copy = pltpu.make_async_copy(prior_hbm, prior_ref, prior_sem)
-    prior_copy.start()
-    rank = rank_of(tm, n_tm)
-    ranks = [rank_of(peer, n_tm) for peer in range(n_tm)]
-    below = sum((rank > other).astype(jnp.int32) for other in ranks)
-    above = sum((rank < other).astype(jnp.int32) for other in ranks)
-    for peer, other in enumerate(ranks):
-        tell(barrier, peer, rank < other)
+    peers = orders(tm, n_tm)
+    below = sum(earlier.astype(jnp.int32) for _, earlier, _ in peers)
+    above = sum(later.astype(jnp.int32) for _, _, later in peers)
+    for peer, _, later in peers:
+        tell(barrier, peer, later)
 
     tiles[...] = jnp.zeros_like(tiles)
 
@@ -146,17 +155,19 @@
     pl.semaphore_wait(barrier, n_sky - 1 + below)
     for peer, there in sends:
         pltpu.make_async_remote_copy(
-            src_ref=table.at[sky],
+            src_ref=mine,
             dst_ref=table.at[sky],
-            send_sem=att_send,
+            send_sem=send_sem,
             recv_sem=att_recv.at[there],
             device_id={"sky": peer},
             device_id_type=MESH,
         ).start()
-    for peer, other in enumerate(ranks):
-        tell(met, peer, rank > other)
+    for peer, earlier, _ in peers:
+        tell(met, peer, earlier)
 
     pltpu.make_async_copy(ints, ints, int_sem).wait()
+    prior_copy = pltpu.make_async_copy(prior_hbm, prior_ref, int_sem)
+    prior_copy.start()
     lane = lax.broadcasted_iota(jnp.int32, (SUBS, LANES), 1)
     sub = lax.broadcasted_iota(jnp.int32, (SUBS, LANES), 0)
     count = []
@@ -224,21 +235,20 @@
             there = highs + (lows >= LANES - i).astype(jnp.int32) if i else highs
             masked[i] = jnp.where(there == chunk, weight[i], 0.0)
 
-    def rows_of(source, p):
-        here = table[source, :, p * LANES : (p + 1) * LANES]
+    def rows_of(source, p, first):
+        at = slice(p * LANES, (p + 1) * LANES)
+        here = mine[:, at] if first else table[source, :, at]
         return [here] + [pltpu.roll(here, LANES - i, 1) for i in range(1, 4)]
 
     def gather(shifted, v, carry):
         at = slice(v * SUBS, v * SUBS + SUBS)
         index = low[at, :]
-        scale = [masked[i, at, :] for i in range(4)]
-        got = []
-        for m in range(4):
-            value = carry[m] if carry else None
-            for i in range(4):
-                term = lane_gather(shifted[i][m : m + 1, :], index) * scale[i]
-                value = term if value is None else value + term
-            got.append(value)
+        got = list(carry) if carry else [None] * 4
+        for i in range(4):
+            scale = masked[i, at, :]
+            for m in range(4):
+                term = lane_gather(shifted[i][m : m + 1, :], index) * scale
+                got[m] = term if got[m] is None else got[m] + term
         return got
 
     pieces = [(sky, None, p) for p in range(per)]
@@ -246,10 +256,13 @@
         pieces += [(source, here if p == 0 else None, p) for p in range(per)]
     for n, (source, here, p) in enumerate(pieces):
         mask_weights(source * per + p)
+        if n + 1 == len(pieces):
+            others = table.at[: n_sky - 1]
+            pltpu.make_async_copy(others, others, send_sem).wait()
         if here is not None:
             arrived = table.at[source]
             pltpu.make_async_copy(arrived, arrived, att_recv.at[here]).wait()
-        shifted = rows_of(source, p)
+        shifted = rows_of(source, p, n < per)
         if n + 1 < len(pieces):
             for v in range(rows // SUBS):
                 at = slice(v * SUBS, v * SUBS + SUBS)
@@ -284,43 +297,40 @@
         groups = [fold_subs(line[i : i + SUBS], sub) for i in range(0, SUMS, SUBS)]
         groups += [jnp.zeros_like(groups[0])] * (ROWS // SUBS - len(groups))
         stacked.append(jnp.concatenate(groups, axis=0))
-    split = [split2(value) for value in stacked]
-    packed = jnp.concatenate([s[k] for k in range(2) for s in split], axis=1)
-    normal = lax.dot_general(
-        member[...], packed, (((1,), (1,)), ((), ())), preferred_element_type=jnp.float32
-    )
-    tiles[:, :, :ROWS] = normal.reshape(n_tm, owned, ROWS)
+    for h, value in enumerate(stacked):
+        for k, part in enumerate(split2(value)):
+            at = (k * halves + h) * LANES
+            packed[:, at : at + LANES] = part
 
     @pl.when(above > 0)
     def _():
         pl.semaphore_wait(met, above)
+
+    normal = lax.dot_general(
+        member[...], packed[...], (((1,), (1,)), ((), ())), preferred_element_type=jnp.float32
+    )
+    tiles[:, :, :ROWS] = normal.reshape(n_tm, owned, ROWS)
 
     for d in range(1, n_tm):
         peer = lax.rem(tm + d, n_tm)
         pltpu.make_async_remote_copy(
             src_ref=tiles.at[peer],
             dst_ref=landed.at[d - 1],
-            send_sem=sum_send,
+            send_sem=send_sem,
             recv_sem=sum_recv,
             device_id={"tm": peer},
             device_id_type=MESH,
         ).start()
     prior_copy.wait()
-    others = table.at[: n_sky - 1]
-    pltpu.make_async_copy(others, others, att_send).wait()
     total = tiles[tm]
     pltpu.make_async_copy(landed, landed, sum_recv).wait()
     for d in range(1, n_tm):
         total = total + landed[d - 1]
-    out_ref[...] = total
-    pltpu.make_async_copy(landed, landed, sum_send).wait()
-
-
-def solve_kernel(total_ref, prior_ref, out_ref, turned):
-    turned[...] = jnp.transpose(total_ref[...])[:ROWS]
-    result = solve_rows(lambda i: turned[i : i + 1, :], lambda i: prior_ref[i : i + 1, :])
+    flat[...] = jnp.transpose(total)[:ROWS]
+    result = solve_rows(lambda i: flat[i : i + 1, :], lambda i: prior_ref[i : i + 1, :])
     for i in range(5):
         out_ref[i : i + 1, :] = result[i]
+    pltpu.make_async_copy(landed, landed, send_sem).wait()
 
 
 def on_device(n_sky, n_tm, attitude, time, parallax, observed, phase, knot, source, count, prior):
@@ -333,12 +343,13 @@
     vmem = pltpu.VMEM
     f32, i32, bf16 = jnp.float32, jnp.int32, jnp.bfloat16
     halves = (LANES // span) // (LANES // rows)
-    total, prior_near = pl.pallas_call(
+    return pl.pallas_call(
         functools.partial(kernel, n_sky, n_tm, span),
-        out_shape=(pltpu.VMEM((owned, LANES), f32), pltpu.VMEM(prior.shape, f32)),
+        out_shape=pltpu.VMEM(prior.shape, f32),
         in_specs=[pl.BlockSpec(memory_space=pl.ANY)] * 9,
-        out_specs=(pl.BlockSpec(memory_space=pltpu.VMEM),) * 2,
+        out_specs=pl.BlockSpec(memory_space=pltpu.VMEM),
         scratch_shapes=[
+            vmem((4, knots), f32),
             vmem((n_sky, 4, knots), f32),
             vmem((4,) + shape, f32),
             vmem((rows + 2 * (blocks // LANES), LANES), i32),
@@ -353,10 +364,11 @@
             vmem((n_tm, owned, LANES), f32),
             vmem((n_tm - 1, owned, LANES), f32),
         ]
-        + [pltpu.SemaphoreType.DMA] * 5
-        + [pltpu.SemaphoreType.DMA((n_sky,))]
-        + [pltpu.SemaphoreType.DMA] * 2
-        + [pltpu.SemaphoreType.REGULAR],
+        + [pltpu.SemaphoreType.DMA] * 3
+        + [pltpu.SemaphoreType.DMA((n_sky - 1,))]
+        + [pltpu.SemaphoreType.DMA]
+        + [pltpu.SemaphoreType.REGULAR]
+        + [vmem(prior.shape, f32), vmem((ROWS, owned), f32), vmem((ROWS, 2 * blocks), bf16)],
         compiler_params=pltpu.CompilerParams(collective_id=0, has_side_effects=True),
     )(
         attitude.reshape(4, knots),
@@ -369,15 +381,6 @@
         count.reshape(blocks // LANES, LANES),
         prior,
     )
-    return pl.pallas_call(
-        solve_kernel,
-        out_shape=jax.ShapeDtypeStruct(prior.shape, f32),
-        in_specs=[pl.BlockSpec(memory_space=pltpu.VMEM)] * 2,
-        scratch_shapes=[vmem((ROWS, owned), f32)],
-    )(
-        pltpu.with_memory_space_constraint(total, pltpu.VMEM),
-        pltpu.with_memory_space_constraint(prior_near, pltpu.VMEM),
-    )
 
 
 def solution(mesh):

time: 12.9 us -> 12.8 us (level)
  Pallas kernels: 12.7 us -> 12 us
  local copies, waits for them, and re-layouts: 0 us -> 0.6 us
    pallas_call x2 -> x1, Pallas kernels: 12.7 us -> 12 us  [on_device(): pl.pallas_call(functools.partial(kernel, n_sky, n_tm, span), out_shape=pl...]
    unnamed x0 -> x1, local copies, waits for them, and re-layouts: none -> 0.6 us
where the time goes in v3:
time: 12.8 us; the launch traced here: 12.6 us
  Pallas kernels  12 us (94%)
  local copies, waits for them, and re-layouts  0.6 us (5%)
    pallas_call x1, Pallas kernels, on_device(): pl.pallas_call(functools.partial(kernel, n_sky, n_tm, span), out_shape=pl...  12 us
    unnamed x1, local copies, waits for them, and re-layouts  0.6 us

profile of v3, /device:TPU:0, one launch (start us, length us, event | category | flops | bytes accessed | tf_op | source)
XLA Modules:
  0.0 12.6 jit_solution(5689908203002200739)
XLA Ops:
  0.0 12.0 %shard_map.91 = f32[5,8]{1,0:T(8,128)S(1)} custom-call(f32[4,128]{1,0:T(4,128)} %bitcast.13, f32[64,128]{1,0:T(8,128)} %bitcast.8, f32[64,128]{1,0:T(8,128)} %bitcast.9, f32[64,128]{1,0:T(8,128)} %bitcast.10, f32[64,128]{1,0:T(8,128)} %bitcast.11, s32[64,128]{1,0:T(8,128)} %bitcast.12, s32[2,128]{1,0:T(2,128)} %bitcast.14, s32[2,128]{1,0:T(2,128)} %bitcast.15, ...), custom_call_target="tpu_custom_call" | custom-call | tf_op jit(solution)/shard_map/pallas_call | solution.py:346
  12.0 0.6 %copy.11 = f32[5,8]{1,0:T(8,128)} copy(f32[5,8]{1,0:T(8,128)S(1)} %shard_map.91) | data formatting | bytes 320

commit v4 on v3

--- a/solution.py
+++ b/solution.py
@@ -89,10 +89,11 @@
     return sends + [(mate, 0)], arrivals
 
 
-def tell(semaphore, peer, exists):
+def tell(semaphore, sky, peer, exists):
     @pl.when(exists)
     def _():
-        pl.semaphore_signal(semaphore, inc=1, device_id={"tm": peer}, device_id_type=MESH)
+        there = {"sky": sky, "tm": peer}
+        pl.semaphore_signal(semaphore, inc=1, device_id=there, device_id_type=MESH)
 
 
 def fold_subs(values, sub):
@@ -116,7 +117,7 @@
     source_hbm, count_hbm, prior_hbm,
     out_ref,
     mine, table, reals, ints, low, high, weight, masked, fact, quat, square, member, tiles, landed,
-    real_sem, int_sem, send_sem, att_recv, sum_recv, met, prior_ref, flat, packed,
+    real_sem, int_sem, send_sem, prior_sem, slot_recv, att_recv, sum_recv, met, got_reals, got_ints, prior_ref, flat, packed,
 ):
     own = pltpu.make_async_copy(attitude_hbm, mine, send_sem)
     own.start()
@@ -146,13 +147,15 @@
     peers = orders(tm, n_tm)
     below = sum(earlier.astype(jnp.int32) for _, earlier, _ in peers)
     above = sum(later.astype(jnp.int32) for _, _, later in peers)
+    mate = sky + 1 - 2 * (sky % 2)
     for peer, _, later in peers:
-        tell(barrier, peer, later)
+        tell(barrier, sky, peer, later)
+        tell(barrier, mate, peer, later)
 
     tiles[...] = jnp.zeros_like(tiles)
 
     own.wait()
-    pl.semaphore_wait(barrier, n_sky - 1 + below)
+    pl.semaphore_wait(barrier, n_sky - 1 + 2 * below)
     for peer, there in sends:
         pltpu.make_async_remote_copy(
             src_ref=mine,
@@ -162,12 +165,23 @@
             device_id={"sky": peer},
             device_id_type=MESH,
         ).start()
+    loaded = ((ints, got_ints, int_sem), (reals, got_reals, real_sem))
+    for k, (here, there, semaphore) in enumerate(loaded):
+        pltpu.make_async_copy(here, here, semaphore).wait()
+        pltpu.make_async_remote_copy(
+            src_ref=here,
+            dst_ref=there,
+            send_sem=semaphore,
+            recv_sem=slot_recv.at[k],
+            device_id={"sky": mate},
+            device_id_type=MESH,
+        ).start()
+    prior_copy = pltpu.make_async_copy(prior_hbm, prior_ref, prior_sem)
+    prior_copy.start()
     for peer, earlier, _ in peers:
-        tell(met, peer, earlier)
-
-    pltpu.make_async_copy(ints, ints, int_sem).wait()
-    prior_copy = pltpu.make_async_copy(prior_hbm, prior_ref, int_sem)
-    prior_copy.start()
+        tell(met, mate, peer, earlier)
+
+    pltpu.make_async_copy(got_ints, got_ints, slot_recv.at[0]).wait()
     lane = lax.broadcasted_iota(jnp.int32, (SUBS, LANES), 1)
     sub = lax.broadcasted_iota(jnp.int32, (SUBS, LANES), 0)
     count = []
@@ -181,8 +195,8 @@
                 got = jnp.where(block // LANES == c, lane_gather(ref[c : c + 1, :], block % LANES), got)
             return got
 
-        count.append(of_block(count_v))
-        hit = jnp.broadcast_to(of_block(source_v)[0:1, :], (sources, LANES)) == which
+        count.append(of_block(got_ints.at[rows + wide :]))
+        hit = jnp.broadcast_to(of_block(got_ints.at[rows : rows + wide])[0:1, :], (sources, LANES)) == which
         one = jnp.where(hit, 1.0, 0.0).astype(jnp.bfloat16)
         for k in range(2):
             at = (k * halves + h) * LANES
@@ -193,13 +207,13 @@
         turned = jnp.transpose(jnp.concatenate(parts, axis=0))
         return [turned[h * fold * span : h * fold * span + span, :] for h in range(halves)]
 
-    for h, knot in enumerate(turn(knot_v[...])):
+    for h, knot in enumerate(turn(got_ints[:rows, :])):
         at = slice(h * span, h * span + span)
         low[at, :] = knot % LANES
         high[at, :] = knot // LANES
 
-    pltpu.make_async_copy(reals, reals, real_sem).wait()
-    turned = [turn(ref[...]) for ref in (phase_v, time_v, parallax_v, observed_v)]
+    pltpu.make_async_copy(got_reals, got_reals, slot_recv.at[1]).wait()
+    turned = [turn(got_reals[i]) for i in range(4)]
     for h in range(halves):
         at = slice(h * span, h * span + span)
         u, time, parallax, observed = (t[h] for t in turned)
@@ -259,6 +273,8 @@
         if n + 1 == len(pieces):
             others = table.at[: n_sky - 1]
             pltpu.make_async_copy(others, others, send_sem).wait()
+            pltpu.make_async_copy(ints, ints, int_sem).wait()
+            pltpu.make_async_copy(reals, reals, real_sem).wait()
         if here is not None:
             arrived = table.at[source]
             pltpu.make_async_copy(arrived, arrived, att_recv.at[here]).wait()
@@ -311,21 +327,21 @@
     )
     tiles[:, :, :ROWS] = normal.reshape(n_tm, owned, ROWS)
 
-    for d in range(1, n_tm):
+    for d in (*range(1, n_tm), 0):
         peer = lax.rem(tm + d, n_tm)
         pltpu.make_async_remote_copy(
             src_ref=tiles.at[peer],
-            dst_ref=landed.at[d - 1],
+            dst_ref=landed.at[d],
             send_sem=send_sem,
             recv_sem=sum_recv,
-            device_id={"tm": peer},
+            device_id={"sky": mate, "tm": peer},
             device_id_type=MESH,
         ).start()
     prior_copy.wait()
-    total = tiles[tm]
     pltpu.make_async_copy(landed, landed, sum_recv).wait()
+    total = landed[0]
     for d in range(1, n_tm):
-        total = total + landed[d - 1]
+        total = total + landed[d]
     flat[...] = jnp.transpose(total)[:ROWS]
     result = solve_rows(lambda i: flat[i : i + 1, :], lambda i: prior_ref[i : i + 1, :])
     for i in range(5):
@@ -362,12 +378,14 @@
             vmem((halves, SUBS, LANES), f32),
             vmem((sources, 2 * blocks), bf16),
             vmem((n_tm, owned, LANES), f32),
-            vmem((n_tm - 1, owned, LANES), f32),
+            vmem((n_tm, owned, LANES), f32),
         ]
-        + [pltpu.SemaphoreType.DMA] * 3
+        + [pltpu.SemaphoreType.DMA] * 4
+        + [pltpu.SemaphoreType.DMA((2,))]
         + [pltpu.SemaphoreType.DMA((n_sky - 1,))]
         + [pltpu.SemaphoreType.DMA]
         + [pltpu.SemaphoreType.REGULAR]
+        + [vmem((4,) + shape, f32), vmem((rows + 2 * (blocks // LANES), LANES), i32)]
         + [vmem(prior.shape, f32), vmem((ROWS, owned), f32), vmem((ROWS, 2 * blocks), bf16)],
         compiler_params=pltpu.CompilerParams(collective_id=0, has_side_effects=True),
     )(

time: 12.8 us -> 12.3 us (0.961)
  Pallas kernels: 12 us -> 11.5 us
    pallas_call x1, Pallas kernels: 12 us -> 11.5 us  [on_device(): pl.pallas_call(functools.partial(kernel, n_sky, n_tm, span), out_shape=pl...]
where the time goes in v4:
time: 12.3 us; the launch traced here: 12.1 us
  Pallas kernels  11.5 us (93%)
  local copies, waits for them, and re-layouts  0.6 us (5%)
    pallas_call x1, Pallas kernels, on_device(): pl.pallas_call(functools.partial(kernel, n_sky, n_tm, span), out_shape=pl...  11.5 us
    unnamed x1, local copies, waits for them, and re-layouts  0.6 us

profile of v4, /device:TPU:0, one launch (start us, length us, event | category | flops | bytes accessed | tf_op | source)
XLA Modules:
  0.0 12.1 jit_solution(7277088573073036484)
XLA Ops:
  0.0 11.5 %shard_map.91 = f32[5,8]{1,0:T(8,128)S(1)} custom-call(f32[4,128]{1,0:T(4,128)} %bitcast.13, f32[64,128]{1,0:T(8,128)} %bitcast.8, f32[64,128]{1,0:T(8,128)} %bitcast.9, f32[64,128]{1,0:T(8,128)} %bitcast.10, f32[64,128]{1,0:T(8,128)} %bitcast.11, s32[64,128]{1,0:T(8,128)} %bitcast.12, s32[2,128]{1,0:T(2,128)} %bitcast.14, s32[2,128]{1,0:T(2,128)} %bitcast.15, ...), custom_call_target="tpu_custom_call" | custom-call | tf_op jit(solution)/shard_map/pallas_call | solution.py:362
  11.5 0.6 %copy.11 = f32[5,8]{1,0:T(8,128)} copy(f32[5,8]{1,0:T(8,128)S(1)} %shard_map.91) | data formatting | bytes 320

commit v5 on v4

--- a/solution.py
+++ b/solution.py
@@ -243,43 +243,48 @@
 
     per = table.shape[2] // LANES
 
-    def mask_weights(chunk):
+    def mask_weights(slot, chunk):
         lows, highs = low[...], high[...]
         for i in range(4):
             there = highs + (lows >= LANES - i).astype(jnp.int32) if i else highs
-            masked[i] = jnp.where(there == chunk, weight[i], 0.0)
+            masked[slot, i] = jnp.where(there == chunk, weight[i], 0.0)
 
     def rows_of(source, p, first):
         at = slice(p * LANES, (p + 1) * LANES)
         here = mine[:, at] if first else table[source, :, at]
         return [here] + [pltpu.roll(here, LANES - i, 1) for i in range(1, 4)]
 
-    def gather(shifted, v, carry):
+    def gather(group, v, carry):
         at = slice(v * SUBS, v * SUBS + SUBS)
         index = low[at, :]
         got = list(carry) if carry else [None] * 4
-        for i in range(4):
-            scale = masked[i, at, :]
-            for m in range(4):
-                term = lane_gather(shifted[i][m : m + 1, :], index) * scale
-                got[m] = term if got[m] is None else got[m] + term
+        for slot, shifted in enumerate(group):
+            for i in range(4):
+                scale = masked[slot, i, at, :]
+                for m in range(4):
+                    term = lane_gather(shifted[i][m : m + 1, :], index) * scale
+                    got[m] = term if got[m] is None else got[m] + term
         return got
 
-    pieces = [(sky, None, p) for p in range(per)]
+    pieces = [(sky, None, p, True) for p in range(per)]
     for source, here in arrivals:
-        pieces += [(source, here if p == 0 else None, p) for p in range(per)]
-    for n, (source, here, p) in enumerate(pieces):
-        mask_weights(source * per + p)
-        if n + 1 == len(pieces):
+        pieces += [(source, here if p == 0 else None, p, False) for p in range(per)]
+    ahead = 2 if len(pieces) > 2 else 1
+    groups = [pieces[:ahead]] + [[piece] for piece in pieces[ahead:]]
+    for n, group in enumerate(groups):
+        for slot, (source, here, p, first) in enumerate(group):
+            mask_weights(slot, source * per + p)
+        if n + 1 == len(groups):
             others = table.at[: n_sky - 1]
             pltpu.make_async_copy(others, others, send_sem).wait()
             pltpu.make_async_copy(ints, ints, int_sem).wait()
             pltpu.make_async_copy(reals, reals, real_sem).wait()
-        if here is not None:
-            arrived = table.at[source]
-            pltpu.make_async_copy(arrived, arrived, att_recv.at[here]).wait()
-        shifted = rows_of(source, p, n < per)
-        if n + 1 < len(pieces):
+        for source, here, p, first in group:
+            if here is not None:
+                arrived = table.at[source]
+                pltpu.make_async_copy(arrived, arrived, att_recv.at[here]).wait()
+        shifted = [rows_of(source, p, first) for source, here, p, first in group]
+        if n + 1 < len(groups):
             for v in range(rows // SUBS):
                 at = slice(v * SUBS, v * SUBS + SUBS)
                 got = gather(shifted, v, [quat[m, at, :] for m in range(4)] if n else None)
@@ -292,7 +297,7 @@
         for g in range(steps):
             v = h * steps + g
             at = slice(v * SUBS, v * SUBS + SUBS)
-            carry = [quat[m, at, :] for m in range(4)] if len(pieces) > 1 else None
+            carry = [quat[m, at, :] for m in range(4)] if len(groups) > 1 else None
             q0, q1, q2, q3 = gather(shifted, v, carry)
             cross = (q0 * q0 + q1 * q1) - (q2 * q2 + q3 * q3)
             along = 2.0 * (q1 * q2 + q0 * q3)
@@ -372,7 +377,7 @@
             vmem(shape, i32),
             vmem(shape, i32),
             vmem((4,) + shape, f32),
-            vmem((4,) + shape, f32),
+            vmem((2, 4) + shape, f32),
             vmem((5,) + shape, f32),
             vmem((4,) + shape, f32),
             vmem((halves, SUBS, LANES), f32),

time: 12.3 us -> 12.2 us (level)
  no operation moved by 1% of the time
where the time goes in v5:
time: 12.2 us; the launch traced here: 12.1 us
  Pallas kernels  11.5 us (94%)
  local copies, waits for them, and re-layouts  0.6 us (5%)
    pallas_call x1, Pallas kernels, on_device(): pl.pallas_call(functools.partial(kernel, n_sky, n_tm, span), out_shape=pl...  11.5 us
    unnamed x1, local copies, waits for them, and re-layouts  0.6 us

profile of v5, /device:TPU:0, one launch (start us, length us, event | category | flops | bytes accessed | tf_op | source)
XLA Modules:
  0.0 12.1 jit_solution(16692337798939724726)
XLA Ops:
  0.0 11.5 %shard_map.91 = f32[5,8]{1,0:T(8,128)S(1)} custom-call(f32[4,128]{1,0:T(4,128)} %bitcast.13, f32[64,128]{1,0:T(8,128)} %bitcast.8, f32[64,128]{1,0:T(8,128)} %bitcast.9, f32[64,128]{1,0:T(8,128)} %bitcast.10, f32[64,128]{1,0:T(8,128)} %bitcast.11, s32[64,128]{1,0:T(8,128)} %bitcast.12, s32[2,128]{1,0:T(2,128)} %bitcast.14, s32[2,128]{1,0:T(2,128)} %bitcast.15, ...), custom_call_target="tpu_custom_call" | custom-call | tf_op jit(solution)/shard_map/pallas_call | solution.py:367
  11.5 0.6 %copy.11 = f32[5,8]{1,0:T(8,128)} copy(f32[5,8]{1,0:T(8,128)S(1)} %shard_map.91) | data formatting | bytes 320

commit v6 on v5

--- a/solution.py
+++ b/solution.py
@@ -117,7 +117,7 @@
     source_hbm, count_hbm, prior_hbm,
     out_ref,
     mine, table, reals, ints, low, high, weight, masked, fact, quat, square, member, tiles, landed,
-    real_sem, int_sem, send_sem, prior_sem, slot_recv, att_recv, sum_recv, met, got_reals, got_ints, prior_ref, flat, packed,
+    real_sem, int_sem, send_sem, slot_recv, att_recv, sum_recv, met, got_reals, got_ints, prior_ref, flat, packed,
 ):
     own = pltpu.make_async_copy(attitude_hbm, mine, send_sem)
     own.start()
@@ -176,8 +176,6 @@
             device_id={"sky": mate},
             device_id_type=MESH,
         ).start()
-    prior_copy = pltpu.make_async_copy(prior_hbm, prior_ref, prior_sem)
-    prior_copy.start()
     for peer, earlier, _ in peers:
         tell(met, mate, peer, earlier)
 
@@ -279,6 +277,8 @@
             pltpu.make_async_copy(others, others, send_sem).wait()
             pltpu.make_async_copy(ints, ints, int_sem).wait()
             pltpu.make_async_copy(reals, reals, real_sem).wait()
+            prior_copy = pltpu.make_async_copy(prior_hbm, prior_ref, int_sem)
+            prior_copy.start()
         for source, here, p, first in group:
             if here is not None:
                 arrived = table.at[source]
@@ -344,9 +344,11 @@
         ).start()
     prior_copy.wait()
     pltpu.make_async_copy(landed, landed, sum_recv).wait()
-    total = landed[0]
-    for d in range(1, n_tm):
-        total = total + landed[d]
+    terms = [landed[d] for d in range(n_tm)]
+    while len(terms) > 1:
+        odd = terms[len(terms) // 2 * 2 :]
+        terms = [a + b for a, b in zip(terms[::2], terms[1::2])] + odd
+    total = terms[0]
     flat[...] = jnp.transpose(total)[:ROWS]
     result = solve_rows(lambda i: flat[i : i + 1, :], lambda i: prior_ref[i : i + 1, :])
     for i in range(5):
@@ -385,7 +387,7 @@
             vmem((n_tm, owned, LANES), f32),
             vmem((n_tm, owned, LANES), f32),
         ]
-        + [pltpu.SemaphoreType.DMA] * 4
+        + [pltpu.SemaphoreType.DMA] * 3
         + [pltpu.SemaphoreType.DMA((2,))]
         + [pltpu.SemaphoreType.DMA((n_sky - 1,))]
         + [pltpu.SemaphoreType.DMA]

time: 12.2 us -> 12.2 us (level)
  no operation moved by 1% of the time
where the time goes in v6:
time: 12.2 us; the launch traced here: 12.1 us
  Pallas kernels  11.4 us (93%)
  local copies, waits for them, and re-layouts  0.6 us (5%)
    pallas_call x1, Pallas kernels, on_device(): pl.pallas_call(functools.partial(kernel, n_sky, n_tm, span), out_shape=pl...  11.4 us
    unnamed x1, local copies, waits for them, and re-layouts  0.6 us

profile of v6, /device:TPU:0, one launch (start us, length us, event | category | flops | bytes accessed | tf_op | source)
XLA Modules:
  0.0 12.1 jit_solution(18391433558051906719)
XLA Ops:
  0.0 11.4 %shard_map.91 = f32[5,8]{1,0:T(8,128)S(1)} custom-call(f32[4,128]{1,0:T(4,128)} %bitcast.13, f32[64,128]{1,0:T(8,128)} %bitcast.8, f32[64,128]{1,0:T(8,128)} %bitcast.9, f32[64,128]{1,0:T(8,128)} %bitcast.10, f32[64,128]{1,0:T(8,128)} %bitcast.11, s32[64,128]{1,0:T(8,128)} %bitcast.12, s32[2,128]{1,0:T(2,128)} %bitcast.14, s32[2,128]{1,0:T(2,128)} %bitcast.15, ...), custom_call_target="tpu_custom_call" | custom-call | tf_op jit(solution)/shard_map/pallas_call | solution.py:369
  11.5 0.6 %copy.11 = f32[5,8]{1,0:T(8,128)} copy(f32[5,8]{1,0:T(8,128)S(1)} %shard_map.91) | data formatting | bytes 320

commit v7 on v6

--- a/solution.py
+++ b/solution.py
@@ -84,7 +84,7 @@
         for bit in [1 << i for i in range(1, n_sky.bit_length())]:
             if 2 * k & bit:
                 base = base + bit * (1 - 2 * ((sky // bit) % 2))
-        sends += [(base, 2 * k - 1 + core), (base + 1, 2 * k - 1 + core)]
+        sends += [(base + 1, 2 * k - 1 + core), (base, 2 * k - 1 + core)]
         arrivals += [(base + 1, 2 * k), (base, 2 * k - 1)]
     return sends + [(mate, 0)], arrivals
 

time: 12.2 us -> 12.2 us (level)
  no operation moved by 1% of the time
where the time goes in v7:
time: 12.2 us; the launch traced here: 12 us
  Pallas kernels  11.4 us (93%)
  local copies, waits for them, and re-layouts  0.6 us (5%)
    pallas_call x1, Pallas kernels, on_device(): pl.pallas_call(functools.partial(kernel, n_sky, n_tm, span), out_shape=pl...  11.4 us
    unnamed x1, local copies, waits for them, and re-layouts  0.6 us

profile of v7, /device:TPU:0, one launch (start us, length us, event | category | flops | bytes accessed | tf_op | source)
XLA Modules:
  0.0 12.0 jit_solution(2110108076819693317)
XLA Ops:
  0.0 11.4 %shard_map.91 = f32[5,8]{1,0:T(8,128)S(1)} custom-call(f32[4,128]{1,0:T(4,128)} %bitcast.13, f32[64,128]{1,0:T(8,128)} %bitcast.8, f32[64,128]{1,0:T(8,128)} %bitcast.9, f32[64,128]{1,0:T(8,128)} %bitcast.10, f32[64,128]{1,0:T(8,128)} %bitcast.11, s32[64,128]{1,0:T(8,128)} %bitcast.12, s32[2,128]{1,0:T(2,128)} %bitcast.14, s32[2,128]{1,0:T(2,128)} %bitcast.15, ...), custom_call_target="tpu_custom_call" | custom-call | tf_op jit(solution)/shard_map/pallas_call | solution.py:369
  11.4 0.6 %copy.11 = f32[5,8]{1,0:T(8,128)} copy(f32[5,8]{1,0:T(8,128)S(1)} %shard_map.91) | data formatting | bytes 320
